TPU v7x, 512 devices: a 8x2x16 block of a 8x8x16 slice. The times are simulated.
512 devices in a mesh: groups: 2 (over y), docs: 16 (over z), mp: 8 (over x), sub: 2 (over core).
Axes of the slice: x: 8, y: 2, z: 16, core: 2. Of those that a mesh axis runs over, the one named last changes fastest.
The devices are a block of a 8x8x16 slice.
Arguments:
- embeddings: bfloat16 [65536, 1024], P(('groups', 'docs', 'mp', 'sub')), parts along dimension 0, may hold values from -6 to 6
- owner_shard: int32 [65536, 1], P(('groups', 'docs', 'mp', 'sub')), parts along dimension 0, may hold values from 0 to 15; in each aligned block of 128 rows (0 to 127, 128 to 255, ...) at most 16 rows name the same one
- query_local: int32 [65536], P(('groups', 'docs', 'mp', 'sub')), parts along dimension 0, may hold values from 0 to 1
- labels: int32 [65536], P(('groups', 'docs', 'mp', 'sub')), parts along dimension 0, may hold values from 0 to 4
- w_first: bfloat16 [1024, 1024], replicated, may hold values from -0.1875 to 0.1875
- w_second: float32 [1024], replicated, may hold values from -0.1875 to 0.1875
Outputs:
- emb_grad: bfloat16 [65536, 1024], P(('groups', 'docs', 'mp', 'sub')), parts along dimension 0
- w_first_grad: float32 [2048, 1024], P(('groups', 'mp', 'sub')), parts along dimension 0
- w_second_grad: float32 [2048], P('groups'), parts along dimension 0
There are 2 independent parts, one for each index of `groups`. A program takes and returns all parts, laid end to end along the dimension named above; an argument that names none is the same for every part. Nothing has to cross between parts.
Inputs may be any that keep to these rules, and one draw needn't show every extreme that they name: `owner_shard`: among the 128 rows of one document shard no owner appears more than 16 times, and some owner appears exactly 16 times.
All inputs are finite; a program needn't handle non-finite values.
Results may differ from a plain program's by a relative error of at most 0.017.
Values may be sent and summed in bfloat16 or wider, within the bound.
No kernel may reach another device: no remote copies, remote signals or barrier semaphores. Data moves between devices by JAX's collectives and lax.ppermute only.
A program may use at most 64 MiB of HBM per device.

v0:
```python
import functools
import math

import jax
import jax.numpy as jnp
from jax import lax
from jax.sharding import PartitionSpec as P

Q_DEV = 2


ranking_softness = 1.0


def one_axis_at_a_time(x, axes):
    return functools.reduce(lax.psum, axes, x)


def split_up(x, dim, count):
    before, after = (x.shape[:dim], x.shape[dim + 1 :])
    return jnp.moveaxis(x.reshape(*before, count, -1, *after), dim, 0)


def summed_on_arrival(x, axis, dim):
    tiles = split_up(x, dim, lax.axis_size(axis))
    arrived = lax.all_to_all(tiles, axis, split_axis=0, concat_axis=0, tiled=True)
    return arrived.astype(jnp.float32).sum(axis=0)


def sent_to_all(x, axis):
    count = lax.axis_size(axis)
    return lax.all_to_all(jnp.broadcast_to(x[None], (count, *x.shape)), axis, 0, 0, tiled=True)


def of_everyone(x, axis):
    return sent_to_all(x, axis).astype(jnp.float32).sum(axis=0)


def silu_slope(pre_act):
    sigmoid_v = jax.nn.sigmoid(pre_act)
    return sigmoid_v * (1.0 + pre_act * (1.0 - sigmoid_v))


def rank_rows(row_start, row_count, scorer_outputs, query_mark, grade_slot):
    slot_index = jnp.arange(scorer_outputs.shape[0], dtype=jnp.int32)
    row_index = row_start + jnp.arange(row_count, dtype=jnp.int32)
    matching_query = (query_mark[:, None] == query_mark[None, :]) & (query_mark[:, None] > 0)
    smooth_rank = (
        jnp.sum(
            jnp.where(
                matching_query,
                jax.nn.sigmoid(
                    (scorer_outputs[None, :] - scorer_outputs[:, None]) / ranking_softness
                ),
                0.0,
            ),
            axis=1,
        )
        - 0.5
    )
    higher = (grade_slot[None, :] > grade_slot[:, None]) | (
        grade_slot[None, :] == grade_slot[:, None]
    ) & (slot_index[None, :] < row_index[:, None])
    ideal_rank = jnp.sum((matching_query & higher).astype(jnp.float32), axis=1)
    row_gain = jnp.exp2(grade_slot.astype(jnp.float32)) - 1.0
    return (smooth_rank, row_gain / jnp.log2(2.0 + ideal_rank))


def lambda_rows(scorer_outputs, query_mark, grade_slot, discount, inv_ideal):
    gain_all = jnp.exp2(grade_slot.astype(jnp.float32)) - 1.0
    matching_query = (query_mark[:, None] == query_mark[None, :]) & (query_mark[:, None] > 0)
    score_gap = scorer_outputs[:, None] - scorer_outputs[None, :]
    weights = (
        jnp.abs(gain_all[:, None] - gain_all[None, :])
        * jnp.abs(discount[:, None] - discount[None, :])
        * inv_ideal[:, None]
    )
    direction = jnp.where(
        grade_slot[:, None] > grade_slot[None, :], -jax.nn.sigmoid(-score_gap), 0.0
    ) + jnp.where(grade_slot[None, :] > grade_slot[:, None], jax.nn.sigmoid(score_gap), 0.0)
    return jnp.sum(jnp.where(matching_query, weights * direction, 0.0), axis=1)


def owner_lambdas(scorer_outputs, query_mark, grade_slot):
    slot_total = scorer_outputs.shape[0]
    row_count = math.gcd(slot_total, 512)
    starts = jnp.arange(0, slot_total, row_count, dtype=jnp.int32)

    def rank_block(first_row):
        return rank_rows(first_row, row_count, scorer_outputs, query_mark, grade_slot)

    smooth_rank, ideal_term = lax.map(rank_block, starts)
    smooth_rank = smooth_rank.reshape(slot_total)
    ideal_term = ideal_term.reshape(slot_total)
    discount = 1.0 / jnp.log2(2.0 + smooth_rank)
    member = (query_mark[:, None] == jnp.arange(1, Q_DEV + 1, dtype=jnp.int32)[None, :]).astype(
        jnp.float32
    )
    per_query = jnp.dot(ideal_term, member, precision=lax.Precision.HIGHEST)
    idcg = jnp.dot(member, per_query, precision=lax.Precision.HIGHEST)
    inv_ideal = jnp.where(idcg > 0.0, 1.0 / jnp.where(idcg > 0.0, idcg, 1.0), 0.0)

    def lambda_block(first_row):
        return lambda_rows(scorer_outputs, query_mark, grade_slot, discount, inv_ideal)

    return lax.map(lambda_block, starts).reshape(slot_total)


def column_product(source, pre_grad):
    return lax.dot_general(
        source, pre_grad, (((0,), (0,)), ((), ())), preferred_element_type=jnp.float32
    )


def weight_grads(inputs, pre_grad, hidden, lambdas):
    second_part = jnp.dot(lambdas, hidden, precision=lax.Precision.HIGHEST)
    second_grad = one_axis_at_a_time(second_part, ("docs", "mp", "sub"))
    lane_part = summed_on_arrival(
        column_product(inputs, pre_grad).astype(jnp.bfloat16), ("mp", "sub"), 0
    )
    first_grad = of_everyone(lane_part.astype(jnp.bfloat16), "docs").astype(jnp.float32)
    return (first_grad, second_grad)


def on_device(embeddings, owner_shard, query_local, labels, w_first, w_second):
    doc_count = lax.axis_size("docs")
    resident_rows = embeddings.shape[0]
    capacity = 2 * resident_rows // doc_count
    slot_count = doc_count * capacity
    target = owner_shard[:, 0]
    owner_hit = (target[:, None] == jnp.arange(doc_count, dtype=jnp.int32)[None, :]).astype(
        jnp.int32
    )
    earlier = jnp.cumsum(owner_hit, axis=0) - owner_hit
    slot_of = target * capacity + jnp.sum(earlier * owner_hit, axis=1)
    query_mark = jnp.zeros((slot_count,), jnp.int32).at[slot_of].set(query_local + 1)
    grade_slot = jnp.zeros((slot_count,), jnp.int32).at[slot_of].set(labels)
    row_info = jnp.stack(
        [query_mark.reshape(doc_count, capacity), grade_slot.reshape(doc_count, capacity)], axis=1
    )
    pre_act = jnp.dot(embeddings, w_first, preferred_element_type=jnp.float32)
    hidden = pre_act * jax.nn.sigmoid(pre_act)
    own_scores = jnp.dot(hidden, w_second, precision=lax.Precision.HIGHEST)
    outgoing = (
        jnp.zeros((slot_count,), jnp.float32)
        .at[slot_of]
        .set(own_scores)
        .reshape(doc_count, capacity)
    )
    incoming, info_in = (
        lax.all_to_all(outgoing, "docs", split_axis=0, concat_axis=0, tiled=True),
        lax.all_to_all(row_info, "docs", split_axis=0, concat_axis=0, tiled=True),
    )
    slot_lambdas = owner_lambdas(
        incoming.reshape(slot_count),
        info_in[:, 0, :].reshape(slot_count),
        info_in[:, 1, :].reshape(slot_count),
    )
    gathered_back = lax.all_to_all(
        slot_lambdas.reshape(doc_count, capacity), "docs", split_axis=0, concat_axis=0, tiled=True
    )
    lambdas = gathered_back.reshape(slot_count)[slot_of]
    pre_grad = (lambdas[:, None] * w_second[None, :] * silu_slope(pre_act)).astype(jnp.bfloat16)
    emb_grad = lax.dot_general(
        pre_grad, w_first, (((1,), (1,)), ((), ())), preferred_element_type=jnp.float32
    ).astype(jnp.bfloat16)
    w_first_grad, w_second_grad = weight_grads(embeddings, pre_grad, hidden, lambdas)
    return (emb_grad, w_first_grad, w_second_grad)


def solution(mesh):
    return jax.shard_map(
        on_device,
        mesh=mesh,
        in_specs=(
            P(("groups", "docs", "mp", "sub"), None),
            P(("groups", "docs", "mp", "sub"), None),
            P(("groups", "docs", "mp", "sub")),
            P(("groups", "docs", "mp", "sub")),
            P(),
            P(),
        ),
        out_specs=(
            P(("groups", "docs", "mp", "sub"), None),
            P(("groups", "mp", "sub"), None),
            P("groups"),
        ),
        check_vma=False,
    )
```

profile of v0, /device:TPU:80, one launch (start us, length us, event | category | flops | bytes accessed | tf_op | source)
XLA Modules:
  0.0 304.0 jit_solution(15351514070500478508)
XLA Ops:
  0.7 0.9 fusion.22
  1.7 0.8 select_reduce_fusion.1
  3.2 1.4 fusion.35
  5.3 1.0 scatter_custom_fusion.2
  6.9 43.7 %all-to-all-start.1 = ((f32[16,1,16]{2,1,0:T(1,128)}), f32[16,1,16]{2,1,0:T(1,128)S(1)}, u32[]{:S(2)}, u32[]{:S(2)}) async-start(f32[16,1,16]{2,1,0:T(1,128)} %all_to_all.22), calls=%async_computation.1 | async-start | bytes 16384 | tf_op jit(solution)/shard_map/all_to_all | solution.py:151
  50.7 1.0 scatter_custom_fusion
  51.6 1.1 scatter_custom_fusion.1
  53.6 9.3 %all-to-all-done.1 = f32[16,1,16]{2,1,0:T(1,128)S(1)} async-done(((f32[16,1,16]{2,1,0:T(1,128)}), f32[16,1,16]{2,1,0:T(1,128)S(1)}, u32[]{:S(2)}, u32[]{:S(2)}) %all-to-all-start.1) | async-done | bytes 1056 | tf_op jit(solution)/shard_map/all_to_all | solution.py:151
  62.8 3.9 %all-to-all-start = ((s32[16,2,16]{2,1,0:T(2,128)}), s32[16,2,16]{2,1,0:T(2,128)S(1)}, u32[]{:S(2)}, u32[]{:S(2)}) async-start(s32[16,2,16]{2,1,0:T(2,128)} %pad_add_fusion), calls=%async_computation | async-start | bytes 32768 | tf_op jit(solution)/shard_map/all_to_all | solution.py:152
  68.0 10.8 %all-to-all-done = s32[16,2,16]{2,1,0:T(2,128)S(1)} async-done(((s32[16,2,16]{2,1,0:T(2,128)}), s32[16,2,16]{2,1,0:T(2,128)S(1)}, u32[]{:S(2)}, u32[]{:S(2)}) %all-to-all-start) | async-done | bytes 2080 | tf_op jit(solution)/shard_map/all_to_all | solution.py:152
  80.3 0.7 all_to_all.24
  81.0 3.9 %all-to-all-start.2 = ((f32[16,1,16]{2,1,0:T(1,128)}), f32[16,1,16]{2,1,0:T(1,128)S(1)}, u32[]{:S(2)}, u32[]{:S(2)}) async-start(f32[16,1,16]{2,1,0:T(1,128)} %all_to_all.24), calls=%async_computation.2 | async-start | bytes 16384 | tf_op jit(solution)/shard_map/all_to_all | solution.py:159
  85.0 11.9 %all-to-all-done.2 = f32[16,1,16]{2,1,0:T(1,128)S(1)} async-done(((f32[16,1,16]{2,1,0:T(1,128)}), f32[16,1,16]{2,1,0:T(1,128)S(1)}, u32[]{:S(2)}, u32[]{:S(2)}) %all-to-all-start.2) | async-done | bytes 1056 | tf_op jit(solution)/shard_map/all_to_all | solution.py:159
  97.7 1.3 gather_fusion
  98.9 0.8 convolution_convert_fusion
  99.8 57.0 %all_to_all.33 = bf16[16,64,1024]{2,1,0:T(8,128)(2,1)} all-to-all(bf16[16,64,1024]{2,1,0:T(8,128)(2,1)S(1)} %bitcast.32), channel_id=1, replica_groups=mesh['groups'=2,'docs'=16,'mp'=8,'sub'=2] {'mp','sub'}, dimensions={0} | all-to-all | bytes 4194304 | tf_op jit(solution)/shard_map/all_to_all | solution.py:26
  156.7 2.0 reduce_sum.67
  158.7 1.6 broadcast_in_dim.48
  160.3 4.8 %all-to-all-start.4 = ((bf16[16,64,1024]{2,1,0:T(8,128)(2,1)}), bf16[16,64,1024]{2,1,0:T(8,128)(2,1)}, u32[]{:S(2)}, u32[]{:S(2)}) async-start(bf16[16,64,1024]{2,1,0:T(8,128)(2,1)} %broadcast_in_dim.48), calls=%async_computation.4 | async-start | bytes 4194304 | tf_op jit(solution)/shard_map/all_to_all | solution.py:32
  165.6 116.3 %psum.21 = f32[1024]{0:T(1024)S(1)} all-reduce(f32[1024]{0:T(1024)S(1)} %bitcast.33), channel_id=1, replica_groups=mesh['groups'=2,'docs'=16,'mp'=8,'sub'=2] {'docs'}, use_global_device_ids=true, to_apply=%region_10.11 | all-reduce | flops 1024 | bytes 8192 | tf_op jit(solution)/shard_map/psum | solution.py:16
  281.9 14.7 %psum.22 = f32[1024]{0:T(1024)S(1)} all-reduce(f32[1024]{0:T(1024)S(1)} %psum.21), channel_id=1, replica_groups=mesh['groups'=2,'docs'=16,'mp'=8,'sub'=2] {'mp'}, use_global_device_ids=true, to_apply=%region_11.12 | all-reduce | flops 1024 | bytes 8192 | tf_op jit(solution)/shard_map/psum | solution.py:16
  296.6 3.1 %psum.23 = f32[1024]{0:T(1024)} all-reduce(f32[1024]{0:T(1024)S(1)} %psum.22), channel_id=1, replica_groups=mesh['groups'=2,'docs'=16,'mp'=8,'sub'=2] {'sub'}, use_global_device_ids=true, to_apply=%region_12.13 | all-reduce | flops 1024 | bytes 8192 | tf_op jit(solution)/shard_map/psum | solution.py:16
  299.7 1.5 convolution_convert_fusion.1
  301.3 2.7 convert_reduce_fusion
  (35 shorter events, 6.9 us)
Async XLA Ops:
  0.6 2.6 copy-start
  0.6 4.0 %copy-start.2 = (f32[1024]{0:T(1024)S(1)}, f32[1024]{0:T(1024)}, u32[]{:S(2)}) copy-start(f32[1024]{0:T(1024)} %param.11) | copy-start | bytes 12292
  3.2 47.4 %copy-start.3 = (s32[128]{0:T(128)S(1)}, s32[128]{0:T(128)}, u32[]{:S(2)}) copy-start(s32[128]{0:T(128)} %param.8) | copy-start | bytes 1540
  4.6 94.3 %copy-start.1 = (bf16[128,1024]{1,0:T(8,128)(2,1)S(1)}, bf16[128,1024]{1,0:T(8,128)(2,1)}, u32[]{:S(2)}) copy-start(bf16[128,1024]{1,0:T(8,128)(2,1)} %param.6) | copy-start | bytes 786436
  6.9 55.9 %all-to-all-start.1 = ((f32[16,1,16]{2,1,0:T(1,128)}), f32[16,1,16]{2,1,0:T(1,128)S(1)}, u32[]{:S(2)}, u32[]{:S(2)}) async-start(f32[16,1,16]{2,1,0:T(1,128)} %all_to_all.22), calls=%async_computation.1 | async-start | bytes 16384 | tf_op jit(solution)/shard_map/all_to_all | solution.py:151
  62.8 16.0 %all-to-all-start = ((s32[16,2,16]{2,1,0:T(2,128)}), s32[16,2,16]{2,1,0:T(2,128)S(1)}, u32[]{:S(2)}, u32[]{:S(2)}) async-start(s32[16,2,16]{2,1,0:T(2,128)} %pad_add_fusion), calls=%async_computation | async-start | bytes 32768 | tf_op jit(solution)/shard_map/all_to_all | solution.py:152
  81.0 15.9 %all-to-all-start.2 = ((f32[16,1,16]{2,1,0:T(1,128)}), f32[16,1,16]{2,1,0:T(1,128)S(1)}, u32[]{:S(2)}, u32[]{:S(2)}) async-start(f32[16,1,16]{2,1,0:T(1,128)} %all_to_all.24), calls=%async_computation.2 | async-start | bytes 16384 | tf_op jit(solution)/shard_map/all_to_all | solution.py:159
  160.3 141.0 %all-to-all-start.4 = ((bf16[16,64,1024]{2,1,0:T(8,128)(2,1)}), bf16[16,64,1024]{2,1,0:T(8,128)(2,1)}, u32[]{:S(2)}, u32[]{:S(2)}) async-start(bf16[16,64,1024]{2,1,0:T(8,128)(2,1)} %broadcast_in_dim.48), calls=%async_computation.4 | async-start | bytes 4194304 | tf_op jit(solution)/shard_map/all_to_all | solution.py:32
where the time goes:
time: 306 us; the launch traced here: 304 us
  blocking collectives  191 us (62%)
  starting transfers between devices  56.3 us (18%)
  waiting for transfers between devices  32 us (10%)
  other arithmetic  10 us (3%)
  local copies, waits for them, and re-layouts  8.37 us (3%)
  matrix products  5.27 us (2%)
    psum x3, blocking collectives, one_axis_at_a_time(): return functools.reduce(lax.psum, axes, x)  134 us
    all_to_all x1, blocking collectives, summed_on_arrival(): lax.all_to_all(tiles, axis, split_axis=0, concat_axis=0, tiled=True)  57 us
    all_to_all x1, starting transfers between devices, on_device(): lax.all_to_all(outgoing, 'docs', split_axis=0, concat_axis=0, tiled=True)  43.7 us
    all_to_all x1, waiting for transfers between devices, on_device(): lax.all_to_all(slot_lambdas.reshape(doc_count, capacity), 'docs', split_a...  11.9 us
    all_to_all x1, waiting for transfers between devices, on_device(): lax.all_to_all(row_info, 'docs', split_axis=0, concat_axis=0, tiled=True)  10.8 us
    all_to_all x1, waiting for transfers between devices, on_device(): lax.all_to_all(outgoing, 'docs', split_axis=0, concat_axis=0, tiled=True)  9.26 us
  transfers between devices with their start and end apart: 4, of which 3 were waited for; matrix products, arithmetic and copies ran while one was open for 2% of the time, Pallas kernels for 0%

commit v1 on v0

v1 whole, which is shorter than its diff:
```python
import functools

import jax
import jax.numpy as jnp
from jax import lax
from jax.experimental import pallas as pl
from jax.experimental.pallas import tpu as pltpu
from jax.sharding import PartitionSpec as P

LANES = 128


def whole(*shape_and_type):
    return jax.ShapeDtypeStruct(*shape_and_type)


def vmem_specs(count):
    return [pl.BlockSpec(memory_space=pltpu.VMEM)] * count


def score_kernel(capacity, emb_ref, w1_ref, w2_ref, owner_ref, query_ref, label_ref, sent_ref, pre_ref, slot_ref):
    rows = emb_ref.shape[0]
    halves = sent_ref.shape[0] // 4
    along = lax.broadcasted_iota(jnp.int32, (rows, rows), 1)
    down = lax.broadcasted_iota(jnp.int32, (rows, rows), 0)

    def column(row):
        return jnp.sum(jnp.where(along == down, row, 0), axis=1, keepdims=True)

    owner = owner_ref[...]
    owner_column = column(owner)
    earlier = jnp.where((owner_column == owner) & (along < down), 1, 0)
    slot = owner_column * capacity + jnp.sum(earlier, axis=1, keepdims=True)
    slot_ref[...] = slot
    mark = column(query_ref[...] + 1).astype(jnp.float32)
    label = column(label_ref[...]).astype(jnp.float32)

    pre_act = jnp.dot(emb_ref[...], w1_ref[...], preferred_element_type=jnp.float32)
    pre_ref[...] = pre_act
    hidden = pre_act * jax.nn.sigmoid(pre_act)
    score = jnp.sum(hidden * w2_ref[...], axis=1, keepdims=True)

    lane = lax.broadcasted_iota(jnp.int32, (rows, LANES), 1)
    sent_ref[...] = jnp.zeros_like(sent_ref)
    for h in range(halves):
        here = slot == lane + h * LANES
        for place, value in enumerate((score, mark, label)):
            sent_ref[place * halves + h : place * halves + h + 1, :] = jnp.sum(
                jnp.where(here, value, 0.0), axis=0, keepdims=True
            )


def within_groups(x, capacity):
    lane = lax.broadcasted_iota(jnp.int32, x.shape, 1)
    out = [x]
    step = capacity // 2
    while step:
        upper = (lane & step) != 0
        spread = []
        for y in out:
            spread.append(jnp.where(upper, pltpu.roll(y, step, 1), y))
            spread.append(jnp.where(upper, y, pltpu.roll(y, LANES - step, 1)))
        out = spread
        step //= 2
    return out


def group_sum(x, capacity):
    lane = lax.broadcasted_iota(jnp.int32, x.shape, 1)
    step = capacity // 2
    while step:
        upper = (lane & step) != 0
        x = x + jnp.where(upper, pltpu.roll(x, step, 1), pltpu.roll(x, LANES - step, 1))
        step //= 2
    return x


def lambda_kernel(
    capacity, part_rows, place_ref, got_ref, pre_ref, slot_ref, w2_ref, emb_ref,
    parts_ref, pre_grad_ref, score_by, mark_by, key_by, disc_by, row_scratch,
):
    sources = got_ref.shape[0]
    halves = got_ref.shape[1] // 4
    me, my_half = place_ref[0], place_ref[1]
    rows = pre_ref.shape[0]
    source = lax.broadcasted_iota(jnp.int32, (sources, LANES), 0)
    lane = lax.broadcasted_iota(jnp.int32, (sources, LANES), 1)
    position = (source * capacity + lane % capacity).astype(jnp.float32)
    slots = float(sources * capacity)
    lane_of_row = lax.broadcasted_iota(jnp.int32, (rows, LANES), 1)
    lambda_column = jnp.zeros((rows, 1), jnp.float32)
    for h in range(halves):
        half_score = got_ref[:, h, :] * 0.5
        mark = got_ref[:, halves + h, :]
        label = got_ref[:, 2 * halves + h, :]
        key = label * slots - position
        for ref, value in ((score_by, half_score), (mark_by, mark), (key_by, key)):
            for c, spread in enumerate(within_groups(value, capacity)):
                ref[c * sources : (c + 1) * sources, :] = spread

        def rank_step(step, sums):
            soft, ideal = sums
            base = pl.multiple_of(step * 8, 8)
            score_rows = score_by[pl.ds(base, 8), :]
            mark_rows = mark_by[pl.ds(base, 8), :]
            key_rows = key_by[pl.ds(base, 8), :]
            for r in range(8):
                same = mark_rows[r : r + 1, :] == mark
                tilt = jnp.tanh(score_rows[r : r + 1, :] - half_score)
                soft = soft + jnp.where(same, tilt + 1.0, 0.0)
                ideal = ideal + jnp.where(same & (key_rows[r : r + 1, :] > key), 1.0, 0.0)
            return soft, ideal

        nothing = jnp.zeros((sources, LANES), jnp.float32)
        soft, ideal = lax.fori_loop(0, capacity * sources // 8, rank_step, (nothing, nothing))
        discount = 1.0 / jnp.log2(2.0 + (0.5 * soft - 0.5))
        gain = jnp.exp2(label) - 1.0
        term = gain / jnp.log2(2.0 + ideal)
        for c, spread in enumerate(within_groups(discount, capacity)):
            disc_by[c * sources : (c + 1) * sources, :] = spread

        for place, value in enumerate((half_score, mark, gain, discount)):
            row_scratch[place * sources : (place + 1) * sources, :] = value
        own_score, own_mark, own_gain, own_disc = (
            row_scratch[pl.ds(place * sources + me, 1), :] for place in range(4)
        )
        ideal_sum = jnp.zeros((1, LANES), jnp.float32)
        for query in range(2):
            asked = query + 1.0
            per_lane = jnp.sum(jnp.where(mark == asked, term, 0.0), axis=0, keepdims=True)
            spread = group_sum(jnp.broadcast_to(per_lane, (8, LANES)), capacity)[:1, :]
            ideal_sum = jnp.where(own_mark == asked, spread, ideal_sum)
        inv_ideal = jnp.where(ideal_sum > 0.0, 1.0 / jnp.where(ideal_sum > 0.0, ideal_sum, 1.0), 0.0)

        total = jnp.zeros((sources, LANES), jnp.float32)
        for c in range(capacity):
            at = slice(c * sources, (c + 1) * sources)
            their_gain = jnp.exp2(jnp.ceil(key_by[at, :] * (1.0 / slots))) - 1.0
            gain_gap = own_gain - their_gain
            gap = 2.0 * (score_by[at, :] - own_score)
            pull = jax.nn.sigmoid(jnp.where(gain_gap > 0.0, gap, -gap))
            pair = -gain_gap * jnp.abs(own_disc - disc_by[at, :]) * pull
            total = total + jnp.where(mark_by[at, :] == own_mark, pair, 0.0)
        lambda_row = jnp.sum(total, axis=0, keepdims=True) * inv_ideal
        here = slot_ref[...] == lane_of_row + h * LANES
        lambda_column = lambda_column + jnp.sum(
            jnp.where(here, lambda_row, 0.0), axis=1, keepdims=True
        )

    pre_act = pre_ref[...]
    gate = jax.nn.sigmoid(pre_act)
    slope = gate * (1.0 + pre_act * (1.0 - gate))
    pre_grad = (lambda_column * w2_ref[...] * slope).astype(jnp.bfloat16)
    pre_grad_ref[...] = pre_grad
    second = jnp.sum(lambda_column * (pre_act * gate), axis=0, keepdims=True)
    columns = pre_act.shape[1] // LANES
    keep_rows = part_rows * columns
    for half in range(2):
        for b in range(parts_ref.shape[1]):
            for k in range(columns):
                parts_ref[half, b, keep_rows + k : keep_rows + k + 1, :] = second[
                    :, k * LANES : (k + 1) * LANES
                ].astype(jnp.bfloat16)
    for b in range(parts_ref.shape[1]):
        product = lax.dot_general(
            emb_ref[:, b * 2 * part_rows : (b + 1) * 2 * part_rows],
            pre_grad,
            (((0,), (0,)), ((), ())),
            preferred_element_type=jnp.float32,
        ).astype(jnp.bfloat16)
        for half in range(2):
            goes_to = (half + my_half) % 2
            for k in range(columns):
                parts_ref[goes_to, b, k * part_rows : (k + 1) * part_rows, :] = product[
                    half * part_rows : (half + 1) * part_rows, k * LANES : (k + 1) * LANES
                ]


def sent_to_all(x, axis):
    count = lax.axis_size(axis)
    return lax.all_to_all(jnp.broadcast_to(x[None], (count, *x.shape)), axis, 0, 0, tiled=True)


def on_device(embeddings, owner_shard, query_local, labels, w_first, w_second):
    docs, lanes, subs = (lax.axis_size(axis) for axis in ("docs", "mp", "sub"))
    rows, width = embeddings.shape
    units = w_first.shape[1]
    capacity = 2 * rows // docs
    halves = docs * capacity // LANES
    w2_row = w_second.reshape(1, units)
    sent, pre_act, slot = pl.pallas_call(
        functools.partial(score_kernel, capacity),
        out_shape=(
            whole((4 * halves, LANES), jnp.float32),
            whole((rows, units), jnp.float32),
            whole((rows, 1), jnp.int32),
        ),
        in_specs=vmem_specs(6),
        out_specs=tuple(vmem_specs(3)),
        name="score",
    )(
        embeddings, w_first, w2_row,
        owner_shard.reshape(1, rows), query_local.reshape(1, rows), labels.reshape(1, rows),
    )
    got = sent_to_all(sent, "docs")

    part_rows = width // (lanes * subs)
    columns = units // LANES
    place = jnp.stack([lax.axis_index("docs"), lax.axis_index("sub")]).astype(jnp.int32)
    parts, pre_grad = pl.pallas_call(
        functools.partial(lambda_kernel, capacity, part_rows),
        out_shape=(
            whole((subs, lanes, (part_rows + 1) * columns, LANES), jnp.bfloat16),
            whole((rows, units), jnp.bfloat16),
        ),
        in_specs=[pl.BlockSpec(memory_space=pltpu.SMEM)] + vmem_specs(5),
        out_specs=tuple(vmem_specs(2)),
        scratch_shapes=[pltpu.VMEM((docs * capacity, LANES), jnp.float32)] * 4
        + [pltpu.VMEM((4 * docs, LANES), jnp.float32)],
        name="lambdas",
    )(place, got, pre_act, slot, w2_row, embeddings)

    other = lax.ppermute(parts[1], "sub", [(0, 1), (1, 0)])
    emb_grad = lax.dot_general(
        pre_grad, w_first, (((1,), (1,)), ((), ())), preferred_element_type=jnp.float32
    ).astype(jnp.bfloat16)
    chip_sum = (parts[0].astype(jnp.float32) + other.astype(jnp.float32)).astype(jnp.bfloat16)
    arrived = lax.all_to_all(chip_sum, "mp", 0, 0, tiled=True)
    line_sum = arrived.astype(jnp.float32).sum(axis=0).astype(jnp.bfloat16)
    first_rows = part_rows * columns
    tiles = line_sum[:first_rows].reshape(docs, first_rows // docs, LANES)
    second = jnp.broadcast_to(line_sum[first_rows:][None], (docs, columns, LANES))
    arrived = lax.all_to_all(jnp.concatenate([tiles, second], axis=1), "docs", 0, 0, tiled=True)
    shard_sum = arrived.astype(jnp.float32).sum(axis=0)
    w_second_grad = shard_sum[first_rows // docs :].reshape(units)
    spread = sent_to_all(shard_sum[: first_rows // docs].astype(jnp.bfloat16), "docs")
    w_first_grad = (
        spread.reshape(columns, part_rows, LANES).transpose(1, 0, 2).reshape(part_rows, units)
    ).astype(jnp.float32)
    return (emb_grad, w_first_grad, w_second_grad)


def solution(mesh):
    split = ("groups", "docs", "mp", "sub")
    return jax.shard_map(
        on_device,
        mesh=mesh,
        in_specs=(P(split, None), P(split, None), P(split), P(split), P(), P()),
        out_specs=(P(split, None), P(("groups", "mp", "sub"), None), P("groups")),
        check_vma=False,
    )
```

time: 306 us -> 150 us (0.49)
  blocking collectives: 191 us -> 54.2 us
  Pallas kernels: 0 us -> 9.46 us
  other arithmetic: 10 us -> 1.78 us
  waiting for transfers between devices: 32 us -> 25.5 us
  starting transfers between devices: 56.3 us -> 50.4 us
  local copies, waits for them, and re-layouts: 8.37 us -> 4.69 us
    psum x3 -> x0, blocking collectives: 134 us -> none  [one_axis_at_a_time(): return functools.reduce(lax.psum, axes, x)]
    all_to_all x3 -> x0, starting transfers between devices: 51.5 us -> none  [the longest x1 43.7 us: on_device(): lax.all_to_all(outgoing, 'docs', split_axis=0, concat_axis=0, tiled=True)]
    all_to_all x1 -> x2, starting transfers between devices: 4.81 us -> 48.5 us  [sent_to_all(): lax.all_to_all(jnp.broadcast_to(x[None], (count, *x.shape)), axis, 0, 0,...]
    all_to_all x3 -> x0, waiting for transfers between devices: 32 us -> none  [the longest x1 11.9 us: on_device(): lax.all_to_all(slot_lambdas.reshape(doc_count, capacity), 'docs', split_a...]
    all_to_all x1 -> x2, waiting for transfers between devices: 0.01 us -> 22.8 us  [sent_to_all(): lax.all_to_all(jnp.broadcast_to(x[None], (count, *x.shape)), axis, 0, 0,...]
    pallas_call x0 -> x2, Pallas kernels: none -> 9.46 us  [the longest x1 6.6 us: on_device(): pl.pallas_call(functools.partial(lambda_kernel, capacity, part_rows), out...]
    reduce_sum x5 -> x2, other arithmetic: 6.3 us -> 0.18 us  [the longest x1 0.15 us: on_device(): line_sum = arrived.astype(jnp.float32).sum(axis=0).astype(jnp.bfloat16)]
    dot_general x6 -> x0, matrix products: 3.73 us -> none  [the longest x1 1.4 us: on_device(): pre_act = jnp.dot(embeddings, w_first, preferred_element_type=jnp.float32)]
  transfers between devices with their start and end apart: 4 -> 3, of which waited for: 3 -> 3; matrix products, arithmetic and copies ran while one was open for 2% -> 2% of each run, Pallas kernels for 0% -> 0%
where the time goes in v1:
time: 150 us; the launch traced here: 149 us
  blocking collectives  54.2 us (36%)
  starting transfers between devices  50.4 us (34%)
  waiting for transfers between devices  25.5 us (17%)
  Pallas kernels  9.46 us (6%)
  local copies, waits for them, and re-layouts  4.69 us (3%)
  matrix products  2.48 us (2%)
  other arithmetic  1.78 us (1%)
    all_to_all x2, starting transfers between devices, sent_to_all(): lax.all_to_all(jnp.broadcast_to(x[None], (count, *x.shape)), axis, 0, 0,...  48.5 us
    all_to_all x1, blocking collectives, on_device(): arrived = lax.all_to_all(chip_sum, 'mp', 0, 0, tiled=True)  36.6 us
    all_to_all x2, waiting for transfers between devices, sent_to_all(): lax.all_to_all(jnp.broadcast_to(x[None], (count, *x.shape)), axis, 0, 0,...  22.8 us
    all_to_all x1, blocking collectives, on_device(): lax.all_to_all(jnp.concatenate([tiles, second], axis=1), 'docs', 0, 0, ti...  17.6 us
    pallas_call x1, Pallas kernels, on_device(): pl.pallas_call(functools.partial(lambda_kernel, capacity, part_rows), out...  6.6 us
  transfers between devices with their start and end apart: 3, of which 3 were waited for; matrix products, arithmetic and copies ran while one was open for 2% of the time, Pallas kernels for 0%

profile of v1, /device:TPU:80, one launch (start us, length us, event | category | flops | bytes accessed | tf_op | source)
XLA Modules:
  0.0 149.3 jit_solution(5375541182076420420)
XLA Ops:
  0.6 2.9 %score.1 = (f32[8,128]{1,0:T(8,128)}, f32[128,1024]{1,0:T(8,128)}, s32[128,1]{1,0:T(8,128)}) custom-call(bf16[128,1024]{1,0:T(8,128)(2,1)} %emb_ref.3, bf16[1024,1024]{1,0:T(8,128)(2,1)} %w1_ref.1, f32[1,1024]{1,0:T(1,128)} %bitcast.30, s32[1,128]{1,0:T(1,128)} %bitcast.32, s32[1,128]{1,0:T(1,128)} %bitcast.33, s32[1,128]{1,0:T(1,128)} %bitcast.34), custom_call_target="tpu_custom_call" | custom-call | tf_op jit(solution)/shard_map/score/pallas_call | solution.py:191
  3.5 1.3 broadcast_in_dim.6
  4.8 43.7 %all-to-all-start = ((f32[16,8,128]{2,1,0:T(8,128)}), f32[16,8,128]{2,1,0:T(8,128)S(1)}, u32[]{:S(2)}, u32[]{:S(2)}) async-start(f32[16,8,128]{2,1,0:T(8,128)} %broadcast_in_dim.6), calls=%async_computation | async-start | bytes 131072 | tf_op jit(solution)/shard_map/all_to_all | solution.py:181
  48.5 0.6 pad_add_fusion.place_ref
  49.1 12.1 %all-to-all-done.got_ref = f32[16,8,128]{2,1,0:T(8,128)S(1)} async-done(((f32[16,8,128]{2,1,0:T(8,128)}), f32[16,8,128]{2,1,0:T(8,128)S(1)}, u32[]{:S(2)}, u32[]{:S(2)}) %all-to-all-start) | async-done | bytes 65568 | tf_op jit(solution)/shard_map/all_to_all | solution.py:181
  61.2 0.0 copy-start.2
  61.2 0.6 copy-done.2
  61.8 6.6 %lambdas.1 = (bf16[2,8,520,128]{3,2,1,0:T(8,128)(2,1)}, bf16[128,1024]{1,0:T(8,128)(2,1)}) custom-call(s32[2]{0:T(128)} %pad_add_fusion.place_ref, f32[16,8,128]{2,1,0:T(8,128)} %copy-done.2, f32[128,1024]{1,0:T(8,128)} %get-tuple-element.9.pre_ref, s32[128,1]{1,0:T(8,128)} %get-tuple-element.10.slot_ref, f32[1,1024]{1,0:T(1,128)} %bitcast.31, ...), custom_call_target="tpu_custom_call" | custom-call | tf_op jit(solution)/shard_map/lambdas/pallas_call | solution.py:210
  68.4 1.5 slice_bitcast_fusion
  69.9 2.0 %collective-permute-start = (bf16[8,520,128]{2,1,0:T(8,128)(2,1)S(1)}, bf16[8,520,128]{2,1,0:T(8,128)(2,1)S(1)}, u32[]{:S(2)}, u32[]{:S(2)}) collective-permute-start(bf16[8,520,128]{2,1,0:T(8,128)(2,1)S(1)} %slice_bitcast_fusion), channel_id=1, source_target_pairs={{0,1},{1,0},{2,3},{3,2},{4,5},{5,4},{6,7},{7,6},{8,9},{9,8},{10,11... | collective-permute-start | bytes 3194888 | tf_op jit(solution)/shard_map/ppermute | solution.py:223
  71.8 2.6 %collective-permute-done = bf16[8,520,128]{2,1,0:T(8,128)(2,1)S(1)} collective-permute-done((bf16[8,520,128]{2,1,0:T(8,128)(2,1)S(1)}, bf16[8,520,128]{2,1,0:T(8,128)(2,1)S(1)}, u32[]{:S(2)}, u32[]{:S(2)}) %collective-permute-start) | collective-permute-done | bytes 1064992 | tf_op jit(solution)/shard_map/ppermute | solution.py:223
  74.5 0.0 copy-done.1
  74.5 0.3 fusion
  74.8 0.0 copy-start
  74.8 36.6 %all_to_all.20 = bf16[8,520,128]{2,1,0:T(8,128)(2,1)S(1)} all-to-all(bf16[8,520,128]{2,1,0:T(8,128)(2,1)S(1)} %fusion), channel_id=1, replica_groups=mesh['groups'=2,'docs'=16,'mp'=8,'sub'=2] {'mp'}, dimensions={0} | all-to-all | bytes 2129920 | tf_op jit(solution)/shard_map/all_to_all | solution.py:228
  111.4 0.1 reduce_sum.21
  111.6 17.6 %all_to_all.21 = bf16[16,40,128]{2,1,0:T(8,128)(2,1)S(1)} all-to-all(bf16[16,40,128]{2,1,0:T(8,128)(2,1)S(1)} %pad_maximum_fusion), channel_id=1, replica_groups=mesh['groups'=2,'docs'=16,'mp'=8,'sub'=2] {'docs'}, dimensions={0} | all-to-all | bytes 327680 | tf_op jit(solution)/shard_map/all_to_all | solution.py:233
  129.2 0.7 broadcast_in_dim.8
  129.9 4.8 %all-to-all-start.3 = ((bf16[16,32,128]{2,1,0:T(8,128)(2,1)}), bf16[16,32,128]{2,1,0:T(8,128)(2,1)S(1)}, u32[]{:S(2)}, u32[]{:S(2)}) async-start(bf16[16,32,128]{2,1,0:T(8,128)(2,1)} %broadcast_in_dim.8), calls=%async_computation.3 | async-start | bytes 262144 | tf_op jit(solution)/shard_map/all_to_all | solution.py:181
  134.7 0.0 copy-done
  134.7 2.5 %convolution_convert_fusion = bf16[128,1024]{1,0:T(8,128)(2,1)} fusion(bf16[128,1024]{1,0:T(8,128)(2,1)} %get-tuple-element.11, bf16[1024,1024]{1,0:T(8,128)(2,1)S(1)} %copy-done), kind=kOutput, calls=%fused_computation.2 | convolution fusion | flops 268566528 | bytes 2621440 | tf_op jit(solution)/shard_map/dot_general | solution.py:224
  137.2 0.6 slice_bitcast_fusion.1
  137.8 10.8 %all-to-all-done.3 = bf16[16,32,128]{2,1,0:T(8,128)(2,1)S(1)} async-done(((bf16[16,32,128]{2,1,0:T(8,128)(2,1)}), bf16[16,32,128]{2,1,0:T(8,128)(2,1)S(1)}, u32[]{:S(2)}, u32[]{:S(2)}) %all-to-all-start.3) | async-done | bytes 131104 | tf_op jit(solution)/shard_map/all_to_all | solution.py:181
  148.6 0.7 copy_bitcast_fusion
  (7 shorter events, 0.1 us)
Async XLA Ops:
  4.8 56.4 %all-to-all-start = ((f32[16,8,128]{2,1,0:T(8,128)}), f32[16,8,128]{2,1,0:T(8,128)S(1)}, u32[]{:S(2)}, u32[]{:S(2)}) async-start(f32[16,8,128]{2,1,0:T(8,128)} %broadcast_in_dim.6), calls=%async_computation | async-start | bytes 131072 | tf_op jit(solution)/shard_map/all_to_all | solution.py:181
  61.2 0.6 copy-start.2
  68.4 6.1 %copy-start.1 = (bf16[2,8,520,128]{3,2,1,0:T(8,128)(2,1)S(1)}, bf16[2,8,520,128]{3,2,1,0:T(8,128)(2,1)}, u32[]{:S(2)}) copy-start(bf16[2,8,520,128]{3,2,1,0:T(8,128)(2,1)} %get-tuple-element.12) | copy-start | bytes 6389764
  69.9 4.6 %collective-permute-start = (bf16[8,520,128]{2,1,0:T(8,128)(2,1)S(1)}, bf16[8,520,128]{2,1,0:T(8,128)(2,1)S(1)}, u32[]{:S(2)}, u32[]{:S(2)}) collective-permute-start(bf16[8,520,128]{2,1,0:T(8,128)(2,1)S(1)} %slice_bitcast_fusion), channel_id=1, source_target_pairs={{0,1},{1,0},{2,3},{3,2},{4,5},{5,4},{6,7},{7,6},{8,9},{9,8},{10,11... | collective-permute-start | bytes 3194888 | tf_op jit(solution)/shard_map/ppermute | solution.py:223
  74.8 60.0 %copy-start = (bf16[1024,1024]{1,0:T(8,128)(2,1)S(1)}, bf16[1024,1024]{1,0:T(8,128)(2,1)}, u32[]{:S(2)}) copy-start(bf16[1024,1024]{1,0:T(8,128)(2,1)} %w1_ref.1) | copy-start | bytes 6291460
  129.9 18.6 %all-to-all-start.3 = ((bf16[16,32,128]{2,1,0:T(8,128)(2,1)}), bf16[16,32,128]{2,1,0:T(8,128)(2,1)S(1)}, u32[]{:S(2)}, u32[]{:S(2)}) async-start(bf16[16,32,128]{2,1,0:T(8,128)(2,1)} %broadcast_in_dim.8), calls=%async_computation.3 | async-start | bytes 262144 | tf_op jit(solution)/shard_map/all_to_all | solution.py:181
